TPU v7x, 256 devices: a whole 4x4x8 slice. The times are simulated.
256 devices in a mesh: band: 64 (over x, z_lo, y, core), pw: 4 (over z_hi).
Axes of the slice: x: 4, y: 4, z: 8 (z_hi: 4, z_lo: 2; z = z_hi * 2 + z_lo), core: 2. Of those that a mesh axis runs over, the one named last changes fastest.
Arguments:
- pair_density: bfloat16 [320, 128, 9216], P('band', None, 'pw'), may hold values from -6 to 6
- eigvecs: bfloat16 [2944, 9216], P('band', 'pw'), may hold values from -0.0625 to 0.0625
- screening: bfloat16 [2944, 2944], P('pw'), may hold values from -0.00048828125 to 0.00048828125
- occupation: float32 [128], replicated, may hold values from 0 to 1
- window_start: int32 [320], P('band'), may hold values from 0 to 511, as said below
- window_len: int32 [320], P('band'), may hold values from 1 to 128, as said below
- slot_band: int32 [320], P('band'), may hold values from -1 to 127, as said below
Outputs:
- sigma: float32 [512, 512], P(('band', 'pw'))
Inputs may be any that keep to these rules, and one draw needn't show every extreme that they name: window_start + window_len <= 512 for every slot. `window_len`: some slot has a window of 128 bands. On each index of band the live slots (slot_band >= 0) come first among its 5 slots; each index holds 3 to 5 live slots, and the counts of index i and index i + 64 / 2 add up to 8.
All inputs are finite; a program needn't handle non-finite values.
Results may differ from a plain program's by a relative error of at most 0.0049.
Values may be sent and summed in bfloat16 or wider, within the bound.
A program may use at most 128 MiB of HBM per device.

v0:
```python
import jax
import jax.numpy as jnp
from jax import lax
from jax.sharding import PartitionSpec as P

NB_SIGMA = 512


def from_partner(array, axis, distance):
    return lax.ppermute(array, axis, [(i, i ^ 1 << distance) for i in range(lax.axis_size(axis))])


def in_blocks(array, dim, length):
    lengths = array.shape
    blocks = array.reshape(*lengths[:dim], length, lengths[dim] // length, *lengths[dim + 1 :])
    return jnp.moveaxis(blocks, dim, 0)


def summed_on_arrival(array, axis, dim):
    blocks = in_blocks(array, dim, lax.axis_size(axis))
    arrived = lax.all_to_all(blocks, axis, split_axis=0, concat_axis=0, tiled=True)
    return arrived.astype(jnp.float32).sum(axis=0)


def sum_at_owner(array, axis, dim):
    length = lax.axis_size(axis)
    blocks = lax.all_to_all(in_blocks(array, dim, length), axis, 0, 0, tiled=True)
    return jnp.sum(blocks, axis=0)


def per_device(pair_density, eigvecs, screening, occupation, window_start, window_len, slot_band):
    capacity, block, plane_rows = pair_density.shape
    top_bit = lax.axis_size("band").bit_length() - 2
    live_count = jnp.sum((slot_band >= 0).astype(jnp.int32))
    last = capacity - 1
    spare_meta = jnp.stack([window_start[last], window_len[last], slot_band[last]])
    got_block = from_partner(pair_density[last], "band", top_bit)
    got_meta = from_partner(spare_meta, "band", top_bit)
    taking = live_count == capacity - 2
    kept_density = pair_density[:last]
    density = jnp.where(taking, kept_density.at[last - 1].set(got_block), kept_density)
    starts = jnp.where(
        taking, window_start[:last].at[last - 1].set(got_meta[0]), window_start[:last]
    )
    lengths = jnp.where(taking, window_len[:last].at[last - 1].set(got_meta[1]), window_len[:last])
    band_ids = jnp.where(taking, slot_band[:last].at[last - 1].set(got_meta[2]), slot_band[:last])
    slots = density.shape[0]
    flat = density.reshape(slots * block, plane_rows)
    partial_proj = lax.dot_general(
        flat,
        lax.all_gather(eigvecs, "band", axis=0, tiled=True),
        (((1,), (1,)), ((), ())),
        preferred_element_type=jnp.float32,
    )
    row_ids = jnp.arange(block, dtype=jnp.int32)
    keep_rows = ((row_ids[None, :] < lengths[:, None]) & (band_ids[:, None] >= 0)).astype(
        jnp.float32
    )
    masked = partial_proj * keep_rows.reshape(slots * block, 1)
    share = lax.psum_scatter(masked, "pw", scatter_dimension=1, tiled=True)
    projected = lax.all_gather(share.astype(jnp.bfloat16), "pw", axis=1, tiled=True)
    width = screening.shape[0]
    own_cols = lax.dynamic_slice_in_dim(projected, lax.axis_index("pw") * width, width, 1)
    screened = lax.dot_general(
        projected, screening, (((1,), (1,)), ((), ())), preferred_element_type=jnp.float32
    ).astype(jnp.bfloat16)
    block_sigma = lax.dot_general(
        screened.reshape(slots, block, width),
        own_cols.reshape(slots, block, width),
        (((2,), (2,)), ((0,), (0,))),
        preferred_element_type=jnp.float32,
    )
    band_list = jnp.arange(occupation.shape[0], dtype=jnp.int32)
    weights = 0.5 - jnp.sum(
        jnp.where(band_list[None, :] == band_ids[:, None], occupation[None, :], 0.0), axis=1
    )
    totals = jnp.zeros((NB_SIGMA + block, NB_SIGMA + block), jnp.float32)
    for index in range(slots):
        first = starts[index]
        previous = lax.dynamic_slice(totals, (first, first), (block, block))
        totals = lax.dynamic_update_slice(
            totals, previous + weights[index] * block_sigma[index], (first, first)
        )
    sigma_part = totals[:NB_SIGMA, :NB_SIGMA]
    by_band = summed_on_arrival(sigma_part.astype(jnp.bfloat16), "band", 0)
    return sum_at_owner(by_band, "pw", 0)


def solution(mesh):
    return jax.shard_map(
        per_device,
        mesh=mesh,
        in_specs=(
            P("band", None, "pw"),
            P("band", "pw"),
            P("pw", None),
            P(),
            P("band"),
            P("band"),
            P("band"),
        ),
        out_specs=P(("band", "pw"), None),
        check_vma=False,
    )
```

profile of v0, /device:TPU:1, one launch (start us, length us, event | category | flops | bytes accessed | tf_op | source)
XLA Modules:
  0.0 408.9 jit_solution(6931820106926020516)
XLA Ops:
  7.3 1.3 slice.139
  8.6 1.5 fusion.16
  10.1 2.0 pad_add_fusion
  12.1 3.6 collective-permute-start
  15.7 1.1 slice_bitcast_fusion
  17.1 1.2 slice_bitcast_fusion.1
  18.3 1.3 fusion.14
  22.2 1.2 select_n.61
  24.2 12.2 %collective-permute-done.1 = bf16[128,2304]{1,0:T(8,128)(2,1)S(1)} collective-permute-done((bf16[128,2304]{1,0:T(8,128)(2,1)S(1)}, bf16[128,2304]{1,0:T(8,128)(2,1)S(1)}, u32[]{:S(2)}, u32[]{:S(2)}) %collective-permute-start.1) | collective-permute-done | bytes 589856 | tf_op jit(solution)/shard_map/ppermute | solution.py:10
  36.3 1.2 fusion.4
  37.5 103.1 %all-gather.6.cloned.1.call-done = bf16[64,46,2304]{2,1,0:T(8,128)(2,1)} async-done(((bf16[1,46,2304]{2,1,0:T(8,128)(2,1)}), bf16[64,46,2304]{2,1,0:T(8,128)(2,1)}) %all-gather.6.cloned.1.call-update) | async-done | bytes 13565968 | tf_op jit(solution)/shard_map/all_gather | solution.py:51
  140.7 16.9 %reshape.157 = bf16[2944,2304]{1,0:T(8,128)(2,1)} reshape(bf16[64,46,2304]{2,1,0:T(8,128)(2,1)} %all-gather.6.cloned.1.call-done) | data formatting | bytes 27131904
  157.6 12.1 %convolution_multiply_fusion = f32[512,2944]{0,1:T(8,128)} fusion(bf16[512,2304]{1,0:T(8,128)(2,1)S(1)} %bitcast.53, bf16[2944,2304]{1,0:T(8,128)(2,1)} %reshape.157, f32[512]{0:T(512)S(1)} %convert_bitcast_fusion), kind=kOutput, calls=%fused_computation | convolution fusion | flops 6947274752 | bytes 21956608 | tf_op jit(solution)/shard_map/dot_general | solution.py:49
  169.8 115.1 %reduce-scatter.2.cloned.1.call-done = f32[512,736]{0,1:T(8,128)} async-done(((f32[512,2944]{0,1:T(8,128)}), f32[512,736]{0,1:T(8,128)}) %reduce-scatter.2.cloned.1.call-update) | async-done | bytes 1507344 | tf_op jit(solution)/shard_map/reduce_scatter | solution.py:60
  284.9 2.4 convert_element_type.26
  295.0 51.6 %all-gather.4.cloned.1.call-done = bf16[512,2944]{0,1:T(8,128)(2,1)} async-done(((bf16[512,736]{0,1:T(8,128)(2,1)}), bf16[512,2944]{0,1:T(8,128)(2,1)}) %all-gather.4.cloned.1.call-update) | async-done | bytes 3014672 | tf_op jit(solution)/shard_map/all_gather | solution.py:61
  346.6 1.2 constant_dynamic-slice_fusion
  348.1 5.7 %fusion = bf16[92,4,8,128]{3,2,1,0:T(8,128)(2,1)S(1)} fusion(bf16[736,2944]{1,0:T(8,128)(2,1)} %param.17, bf16[512,2944]{0,1:T(8,128)(2,1)} %all-gather.4.cloned.1.call-done), kind=kOutput, calls=%fused_computation.2 | convolution fusion | flops 2219163648 | bytes 8101888 | tf_op jit(solution)/shard_map/dot_general | solution.py:64
  354.8 2.1 dynamic_update_slice.12
  357.6 2.1 dynamic_update_slice.13
  360.4 2.1 dynamic_update_slice.14
  363.2 2.1 dynamic_update_slice.15
  365.4 26.5 %all_to_all.10 = bf16[64,8,512]{2,1,0:T(8,128)(2,1)S(1)} all-to-all(bf16[64,8,512]{2,1,0:T(8,128)(2,1)S(1)} %fusion.5), channel_id=1, replica_groups=mesh['band'=64,'pw'=4] {'band'}, dimensions={0} | all-to-all | bytes 1048576 | tf_op jit(solution)/shard_map/all_to_all | solution.py:21
  392.0 9.7 %all_to_all.11 = f32[4,2,512]{2,1,0:T(2,128)S(1)} all-to-all(f32[4,2,512]{2,1,0:T(2,128)S(1)} %reshape.154), channel_id=1, replica_groups=mesh['band'=64,'pw'=4] {'pw'}, dimensions={0} | all-to-all | bytes 32768 | tf_op jit(solution)/shard_map/all_to_all | solution.py:27
  (34 shorter events, 7.6 us)
Async XLA Ops:
  6.5 134.1 %all-gather.6.cloned.1.call-start = ((), (), s32[]{:S(2)}) async-start(), calls=%async_computation.5 | async-start | bytes 14376960 | tf_op jit(solution)/shard_map/all_gather | solution.py:51
  7.3 277.6 %reduce-scatter.2.cloned.1.call-start = ((), (), s32[]{:S(2)}) async-start(), calls=%async_computation.3 | async-start | bytes 7536640 | tf_op jit(solution)/shard_map/reduce_scatter | solution.py:60
  12.1 7.5 %copy-start = (s32[5]{0:T(128)S(1)}, s32[5]{0:T(128)}, u32[]{:S(2)}) copy-start(s32[5]{0:T(128)} %param.20) | copy-start | bytes 64
  12.1 24.2 %slice-start = ((bf16[5,128,2304]{2,1,0:T(8,128)(2,1)}), bf16[4,128,2304]{2,1,0:T(8,128)(2,1)S(1)}, s32[]{:S(2)}) async-start(bf16[5,128,2304]{2,1,0:T(8,128)(2,1)} %param.15), calls=%async_computation.6 | async-start | bytes 4718592 | tf_op jit(solution)/shard_map/slice | solution.py:40
  12.1 8.1 %collective-permute-start = (s32[3]{0:T(128)S(1)}, s32[3]{0:T(128)S(1)}, u32[]{:S(2)}, u32[]{:S(2)}) collective-permute-start(s32[3]{0:T(128)S(1)} %pad_add_fusion), channel_id=1, source_target_pairs={{0,128},{4,132},{8,136},{12,140},{16,144},{20,148},{24,152},{28,15... | collective-permute-start | bytes 44 | tf_op jit(solution)/shard_map/ppermute | solution.py:10
  16.9 19.5 %collective-permute-start.1 = (bf16[128,2304]{1,0:T(8,128)(2,1)S(1)}, bf16[128,2304]{1,0:T(8,128)(2,1)S(1)}, u32[]{:S(2)}, u32[]{:S(2)}) collective-permute-start(bf16[128,2304]{1,0:T(8,128)(2,1)S(1)} %slice_bitcast_fusion), channel_id=1, source_target_pairs={{0,128},{4,132},{8,136},{12,140},{16,144},{20,148},{24,152},{28,15... | collective-permute-start | bytes 1769480 | tf_op jit(solution)/shard_map/ppermute | solution.py:10
  169.7 124.5 %copy-start.1 = (f32[128]{0:T(128)S(1)}, f32[128]{0:T(128)}, u32[]{:S(2)}) copy-start(f32[128]{0:T(128)} %param.18) | copy-start | bytes 1540
  169.7 124.5 %copy-start.2 = (s32[4,1]{0,1:T(1,128)S(1)}, s32[4,1]{0,1:T(1,128)}, u32[]{:S(2)}) copy-start(s32[4,1]{0,1:T(1,128)} %select_n.61) | copy-start | bytes 52
  169.7 176.9 %all-gather.4.cloned.1.call-start = ((), (), s32[]{:S(2)}) async-start(), calls=%async_computation.4 | async-start | bytes 3768320 | tf_op jit(solution)/shard_map/all_gather | solution.py:61
Sparse Core Ops, SparseCore 0:
  9.2 131.4 all-gather.5
  169.8 115.0 reduce-scatter.1
  287.4 59.1 all-gather.3
where the time goes:
time: 410 us; the launch traced here: 409 us
  waiting for transfers between devices  283 us (69%)
  blocking collectives  36.3 us (9%)
  local copies, waits for them, and re-layouts  33.8 us (8%)
  between operations  22.1 us (5%)
  matrix products  18.1 us (4%)
  other arithmetic  11.9 us (3%)
    reduce_scatter x1, waiting for transfers between devices, per_device(): share = lax.psum_scatter(masked, 'pw', scatter_dimension=1, tiled=True)  115 us
    all_gather x1, waiting for transfers between devices, per_device(): lax.all_gather(eigvecs, 'band', axis=0, tiled=True)  103 us
    all_gather x1, waiting for transfers between devices, per_device(): lax.all_gather(share.astype(jnp.bfloat16), 'pw', axis=1, tiled=True)  51.6 us
    all_to_all x1, blocking collectives, summed_on_arrival(): lax.all_to_all(blocks, axis, split_axis=0, concat_axis=0, tiled=True)  26.5 us
    unnamed x8, local copies, waits for them, and re-layouts  17 us
    ppermute x2, waiting for transfers between devices, from_partner(): lax.ppermute(array, axis, [(i, i ^ 1 << distance) for i in range(lax.axis...  12.2 us
    dot_general x1, matrix products, per_device(): lax.dot_general(flat, lax.all_gather(eigvecs, 'band', axis=0, tiled=True)...  12.1 us
    all_to_all x1, blocking collectives, sum_at_owner(): lax.all_to_all(in_blocks(array, dim, length), axis, 0, 0, tiled=True)  9.74 us
  transfers between devices with their start and end apart: 5, of which 4 were waited for; matrix products, arithmetic and copies ran while one was open for 3% of the time, Pallas kernels for 0%

commit v1 on v0

--- a/solution.py
+++ b/solution.py
@@ -2,8 +2,15 @@
 import jax.numpy as jnp
 from jax import lax
 from jax.sharding import PartitionSpec as P
+from jax.lax import all_to_all, axis_size
 
 NB_SIGMA = 512
+
+
+def face_prepare(page, out_dim):
+    f_next = axis_size("band")
+    extra = jnp.stack(f_next * [page])
+    return jnp.concatenate(all_to_all(extra, "band", 0, 0), out_dim)
 
 
 def from_partner(array, axis, distance):
@@ -47,10 +54,7 @@
     slots = density.shape[0]
     flat = density.reshape(slots * block, plane_rows)
     partial_proj = lax.dot_general(
-        flat,
-        lax.all_gather(eigvecs, "band", axis=0, tiled=True),
-        (((1,), (1,)), ((), ())),
-        preferred_element_type=jnp.float32,
+        flat, face_prepare(eigvecs, 0), (((1,), (1,)), ((), ())), preferred_element_type=jnp.float32
     )
     row_ids = jnp.arange(block, dtype=jnp.int32)
     keep_rows = ((row_ids[None, :] < lengths[:, None]) & (band_ids[:, None] >= 0)).astype(

time: 410 us -> 497 us (1.21)
  waiting for transfers between devices: 283 us -> 353 us
  starting transfers between devices: 3.95 us -> 14 us
  local copies, waits for them, and re-layouts: 33.8 us -> 39.5 us
    ppermute x2, waiting for transfers between devices: 12.2 us -> 167 us  [from_partner(): lax.ppermute(array, axis, [(i, i ^ 1 << distance) for i in range(lax.axis...]
    all_gather x1 -> x0, waiting for transfers between devices: 103 us -> none  [per_device(): lax.all_gather(eigvecs, 'band', axis=0, tiled=True)]
    reshape x0 -> x1, local copies, waits for them, and re-layouts: none -> 17 us  [face_prepare(): return jnp.concatenate(all_to_all(extra, 'band', 0, 0), out_dim)]
    unnamed x8 -> x15, local copies, waits for them, and re-layouts: 17 us -> 0.03 us
    reduce_scatter x1, waiting for transfers between devices: 115 us -> 128 us  [per_device(): share = lax.psum_scatter(masked, 'pw', scatter_dimension=1, tiled=True)]
    all_to_all x0 -> x1, starting transfers between devices: none -> 10.8 us  [face_prepare(): return jnp.concatenate(all_to_all(extra, 'band', 0, 0), out_dim)]
    all_to_all x0 -> x1, waiting for transfers between devices: none -> 7.53 us  [face_prepare(): return jnp.concatenate(all_to_all(extra, 'band', 0, 0), out_dim)]
    another operation x1 -> x2, local copies, waits for them, and re-layouts: 1.5 us -> 7.64 us  [the longest x1 6.97 us: face_prepare(): extra = jnp.stack(f_next * [page])]
  transfers between devices with their start and end apart: 5 -> 5, of which waited for: 4 -> 5; matrix products, arithmetic and copies ran while one was open for 3% -> 2% of each run, Pallas kernels for 0% -> 0%
where the time goes in v1:
time: 497 us; the launch traced here: 496 us
  waiting for transfers between devices  353 us (71%)
  local copies, waits for them, and re-layouts  39.5 us (8%)
  blocking collectives  36.3 us (7%)
  between operations  22.6 us (5%)
  matrix products  18.1 us (4%)
  starting transfers between devices  14 us (3%)
  other arithmetic  12.1 us (2%)
    ppermute x2, waiting for transfers between devices, from_partner(): lax.ppermute(array, axis, [(i, i ^ 1 << distance) for i in range(lax.axis...  167 us
    reduce_scatter x1, waiting for transfers between devices, per_device(): share = lax.psum_scatter(masked, 'pw', scatter_dimension=1, tiled=True)  128 us
    all_gather x1, waiting for transfers between devices, per_device(): lax.all_gather(share.astype(jnp.bfloat16), 'pw', axis=1, tiled=True)  51.3 us
    all_to_all x1, blocking collectives, summed_on_arrival(): lax.all_to_all(blocks, axis, split_axis=0, concat_axis=0, tiled=True)  26.5 us
    reshape x1, local copies, waits for them, and re-layouts, face_prepare(): return jnp.concatenate(all_to_all(extra, 'band', 0, 0), out_dim)  17 us
    dot_general x1, matrix products, per_device(): lax.dot_general(flat, face_prepare(eigvecs, 0), (((1,), (1,)), ((), ())),...  12 us
    all_to_all x1, starting transfers between devices, face_prepare(): return jnp.concatenate(all_to_all(extra, 'band', 0, 0), out_dim)  10.8 us
  transfers between devices with their start and end apart: 5, of which 5 were waited for; matrix products, arithmetic and copies ran while one was open for 2% of the time, Pallas kernels for 0%

profile of v1, /device:TPU:1, one launch (start us, length us, event | category | flops | bytes accessed | tf_op | source)
XLA Modules:
  0.0 496.0 jit_solution(769066479059651475)
XLA Ops:
  6.5 7.0 %stack.5 = bf16[64,46,2304]{2,1,0:T(8,128)(2,1)} broadcast(bf16[46,2304]{1,0:T(8,128)(2,1)} %param.16), dimensions={1,2} | broadcast | bytes 13777920 | tf_op jit(solution)/shard_map/stack | solution.py:12
  13.5 10.8 %all-to-all-start = ((bf16[64,46,2304]{2,1,0:T(8,128)(2,1)}), bf16[64,46,2304]{2,1,0:T(8,128)(2,1)}, u32[]{:S(2)}, u32[]{:S(2)}) async-start(bf16[64,46,2304]{2,1,0:T(8,128)(2,1)} %stack.5), calls=%async_computation | async-start | bytes 28311552 | tf_op jit(solution)/shard_map/all_to_all | solution.py:13
  25.6 2.0 pad_add_fusion
  27.6 3.0 collective-permute-start
  32.0 1.7 slice.144
  34.3 153.1 %collective-permute-done = s32[3]{0:T(128)S(1)} collective-permute-done((s32[3]{0:T(128)S(1)}, s32[3]{0:T(128)S(1)}, u32[]{:S(2)}, u32[]{:S(2)}) %collective-permute-start) | collective-permute-done | bytes 44 | tf_op jit(solution)/shard_map/ppermute | solution.py:17
  189.4 1.4 select_n.61
  191.6 13.9 %collective-permute-done.1 = bf16[128,2304]{1,0:T(8,128)(2,1)} collective-permute-done((bf16[128,2304]{1,0:T(8,128)(2,1)S(1)}, bf16[128,2304]{1,0:T(8,128)(2,1)}, u32[]{:S(2)}, u32[]{:S(2)}) %collective-permute-start.1) | collective-permute-done | bytes 589856 | tf_op jit(solution)/shard_map/ppermute | solution.py:17
  205.5 2.0 fusion.4
  207.5 7.5 %all-to-all-done = bf16[64,46,2304]{2,1,0:T(8,128)(2,1)} async-done(((bf16[64,46,2304]{2,1,0:T(8,128)(2,1)}), bf16[64,46,2304]{2,1,0:T(8,128)(2,1)}, u32[]{:S(2)}, u32[]{:S(2)}) %all-to-all-start) | async-done | bytes 13565984 | tf_op jit(solution)/shard_map/all_to_all | solution.py:13
  215.1 17.0 %reshape.156 = bf16[2944,2304]{1,0:T(8,128)(2,1)} reshape(bf16[64,46,2304]{2,1,0:T(8,128)(2,1)} %all-to-all-done) | data formatting | bytes 27131904 | tf_op jit(solution)/shard_map/reshape | solution.py:13
  232.0 12.0 %convolution_multiply_fusion = f32[512,2944]{0,1:T(8,128)} fusion(bf16[512,2304]{1,0:T(8,128)(2,1)S(1)} %bitcast.53, bf16[2944,2304]{1,0:T(8,128)(2,1)} %reshape.156, f32[512]{0:T(512)S(1)} %convert_bitcast_fusion), kind=kOutput, calls=%fused_computation | convolution fusion | flops 6947274752 | bytes 21956608 | tf_op jit(solution)/shard_map/dot_general | solution.py:56
  244.2 127.6 %reduce-scatter.2.cloned.1.call-done = f32[512,736]{0,1:T(8,128)} async-done(((f32[512,2944]{0,1:T(8,128)}), f32[512,736]{0,1:T(8,128)}) %reduce-scatter.2.cloned.1.call-update) | async-done | bytes 1507344 | tf_op jit(solution)/shard_map/reduce_scatter | solution.py:64
  371.8 2.4 convert_element_type.26
  382.0 51.3 %all-gather.2.cloned.1.call-done = bf16[512,2944]{0,1:T(8,128)(2,1)} async-done(((bf16[512,736]{0,1:T(8,128)(2,1)}), bf16[512,2944]{0,1:T(8,128)(2,1)}) %all-gather.2.cloned.1.call-update) | async-done | bytes 3014672 | tf_op jit(solution)/shard_map/all_gather | solution.py:65
  433.3 1.2 constant_dynamic-slice_fusion
  434.8 5.7 %fusion = bf16[92,4,8,128]{3,2,1,0:T(8,128)(2,1)S(1)} fusion(bf16[736,2944]{1,0:T(8,128)(2,1)} %param.17, bf16[512,2944]{0,1:T(8,128)(2,1)} %all-gather.2.cloned.1.call-done), kind=kOutput, calls=%fused_computation.2 | convolution fusion | flops 2219163648 | bytes 8101888 | tf_op jit(solution)/shard_map/dot_general | solution.py:68
  441.6 2.1 dynamic_update_slice.12
  444.3 2.1 dynamic_update_slice.13
  447.2 2.1 dynamic_update_slice.14
  449.2 0.7 fusion.7
  450.0 2.1 dynamic_update_slice.15
  452.1 26.5 %all_to_all.15 = bf16[64,8,512]{2,1,0:T(8,128)(2,1)S(1)} all-to-all(bf16[64,8,512]{2,1,0:T(8,128)(2,1)S(1)} %fusion.5), channel_id=1, replica_groups=mesh['band'=64,'pw'=4] {'band'}, dimensions={0} | all-to-all | bytes 1048576 | tf_op jit(solution)/shard_map/all_to_all | solution.py:28
  478.8 9.7 %all_to_all.16 = f32[4,2,512]{2,1,0:T(2,128)S(1)} all-to-all(f32[4,2,512]{2,1,0:T(2,128)S(1)} %reshape.160), channel_id=1, replica_groups=mesh['band'=64,'pw'=4] {'pw'}, dimensions={0} | all-to-all | bytes 32768 | tf_op jit(solution)/shard_map/all_to_all | solution.py:34
  (41 shorter events, 8.7 us)
Async XLA Ops:
  13.5 10.8 %copy-start.4 = (s32[5]{0:T(128)S(1)}, s32[5]{0:T(128)}, u32[]{:S(2)}) copy-start(s32[5]{0:T(128)} %param.20) | copy-start | bytes 64
  13.5 11.5 %copy-start.2 = (s32[5]{0:T(128)S(1)}, s32[5]{0:T(128)}, u32[]{:S(2)}) copy-start(s32[5]{0:T(128)} %param.19) | copy-start | bytes 64
  13.5 11.5 %copy-start.3 = (s32[5]{0:T(128)S(1)}, s32[5]{0:T(128)}, u32[]{:S(2)}) copy-start(s32[5]{0:T(128)} %param.21) | copy-start | bytes 64
  13.5 17.1 %copy-start = (bf16[5,128,2304]{2,1,0:T(8,128)(2,1)S(1)}, bf16[5,128,2304]{2,1,0:T(8,128)(2,1)}, u32[]{:S(2)}) copy-start(bf16[5,128,2304]{2,1,0:T(8,128)(2,1)} %param.15) | copy-start | bytes 8847364
  13.5 201.6 %all-to-all-start = ((bf16[64,46,2304]{2,1,0:T(8,128)(2,1)}), bf16[64,46,2304]{2,1,0:T(8,128)(2,1)}, u32[]{:S(2)}, u32[]{:S(2)}) async-start(bf16[64,46,2304]{2,1,0:T(8,128)(2,1)} %stack.5), calls=%async_computation | async-start | bytes 28311552 | tf_op jit(solution)/shard_map/all_to_all | solution.py:13
  24.3 347.5 %reduce-scatter.2.cloned.1.call-start = ((), (), s32[]{:S(2)}) async-start(), calls=%async_computation.4 | async-start | bytes 7536640 | tf_op jit(solution)/shard_map/reduce_scatter | solution.py:64
  27.6 159.8 %collective-permute-start = (s32[3]{0:T(128)S(1)}, s32[3]{0:T(128)S(1)}, u32[]{:S(2)}, u32[]{:S(2)}) collective-permute-start(s32[3]{0:T(128)S(1)} %pad_add_fusion), channel_id=1, source_target_pairs={{0,128},{4,132},{8,136},{12,140},{16,144},{20,148},{24,152},{28,15... | collective-permute-start | bytes 44 | tf_op jit(solution)/shard_map/ppermute | solution.py:17
  30.7 174.8 %collective-permute-start.1 = (bf16[128,2304]{1,0:T(8,128)(2,1)S(1)}, bf16[128,2304]{1,0:T(8,128)(2,1)}, u32[]{:S(2)}, u32[]{:S(2)}) collective-permute-start(bf16[128,2304]{1,0:T(8,128)(2,1)S(1)} %slice_bitcast_fusion), channel_id=1, source_target_pairs={{0,128},{4,132},{8,136},{12,140},{16,144},{20,148},{24,152},{28,15... | collective-permute-start | bytes 1769480 | tf_op jit(solution)/shard_map/ppermute | solution.py:17
  207.5 24.5 %copy-start.1 = (bf16[4,128,2304]{2,1,0:T(8,128)(2,1)S(1)}, bf16[4,128,2304]{2,1,0:T(8,128)(2,1)}, u32[]{:S(2)}) copy-start(bf16[4,128,2304]{2,1,0:T(8,128)(2,1)} %fusion.4) | copy-start | bytes 7077892
  244.1 137.1 %copy-start.5 = (f32[128]{0:T(128)S(1)}, f32[128]{0:T(128)}, u32[]{:S(2)}) copy-start(f32[128]{0:T(128)} %param.18) | copy-start | bytes 1540
  244.1 137.1 %copy-start.6 = (s32[4,1]{0,1:T(1,128)S(1)}, s32[4,1]{0,1:T(1,128)}, u32[]{:S(2)}) copy-start(s32[4,1]{0,1:T(1,128)} %select_n.61) | copy-start | bytes 52
  244.1 189.2 %all-gather.2.cloned.1.call-start = ((), (), s32[]{:S(2)}) async-start(), calls=%async_computation.5 | async-start | bytes 3768320 | tf_op jit(solution)/shard_map/all_gather | solution.py:65
Sparse Core Ops, SparseCore 0:
  244.2 127.4 reduce-scatter.1
  374.3 59.0 all-gather.1
